TPU v7x, 256 devices: a whole 4x4x8 slice. The times are simulated.
256 devices in a mesh: face: 16 (over z, core), sub: 16 (over y, x).
Axes of the slice: x: 4, y: 4, z: 8, core: 2. Of those that a mesh axis runs over, the one named last changes fastest.
Arguments:
- mesh_latent: bfloat16 [65536, 512], P(('face', 'sub')), may hold values from -6 to 6
- edge_latent: bfloat16 [524288, 512], P(('face', 'sub')), may hold values from -6 to 6
- grid_features: bfloat16 [65536, 384], P(('face', 'sub')), may hold values from -6 to 6
- senders: int32 [524288], P(('face', 'sub')), may hold values from 0 to 383, as said below
- receivers: int32 [524288], P(('face', 'sub')), may hold values from 0 to 255
- send_lists: int32 [256, 4, 32], P(('face', 'sub')), may hold values from -1 to 255, as said below
- link_sources: int32 [131072], P(('face', 'sub')), may hold values from 0 to 255
- link_targets: int32 [131072], P(('face', 'sub')), may hold values from 0 to 255
- node_area: float32 [65536], P(('face', 'sub')), may hold values from 0.25 to 4.5
- grid_weight: bfloat16 [384, 512], P(None, 'sub'), may hold values from -0.3125 to 0.3125
- encode_weight: bfloat16 [1024, 512], P('sub'), may hold values from -0.1875 to 0.1875
- edge_first: bfloat16 [1, 1536, 512], P(None, 'sub'), may hold values from -0.15625 to 0.15625
- edge_second: bfloat16 [1, 512, 512], P(None, 'sub'), may hold values from -0.25 to 0.25
- node_first: bfloat16 [1, 1024, 512], P(None, 'sub'), may hold values from -0.1875 to 0.1875
- node_second: bfloat16 [1, 512, 512], P(None, 'sub'), may hold values from -0.25 to 0.25
Outputs:
- mesh_result: bfloat16 [65536, 512], P(('face', 'sub'))
- edge_result: bfloat16 [524288, 512], P(('face', 'sub'))
- masses: float32 [1, 512], replicated
Inputs may be any that keep to these rules, and one draw needn't show every extreme that they name: `send_lists`: entries are the sending partition's own node numbers, or -1 for an unused slot; in every list the used slots come first, hold distinct nodes and number 32 // 2 or more; for every list number some partition uses all 32 slots. `senders`: A value below 256 names one of the partition's own nodes; 256 + d * 32 + k names slot k of the list with number d that the partition receives, and that slot is always a used one.
All inputs are finite; a program needn't handle non-finite values.
Results may differ from a plain program's by a relative error of at most 0.008.
Values may be sent and summed in bfloat16 or wider, within the bound.
A program may use at most 64 MiB of HBM per device.

v0:
```python
import jax
import jax.numpy as jnp
from jax import lax
from jax.sharding import Mesh
from jax.sharding import PartitionSpec as P

SUB = ("sub_0", "sub_1")
FACE = ("face_0", "face_1")
FACE_SUB = ("face_0", "face_1", "sub_0", "sub_1")


def laid_out(blocks, dim):
    shape = list(blocks.shape[1:])
    shape[dim] *= blocks.shape[0]
    return jnp.moveaxis(blocks, 0, dim).reshape(shape)


def from_everyone(x, axis):
    copies = jnp.broadcast_to(x, (lax.axis_size(axis), *x.shape))
    return lax.all_to_all(copies, axis, split_axis=0, concat_axis=0, tiled=True)


def gathered_copies(x, axis, dim):
    return laid_out(from_everyone(x, axis), dim)


def gather_axes(x, axes, dim):
    for axis in reversed(axes):
        x = lax.all_gather(x, axis, axis=dim, tiled=True)
    return x


def passed_along(value, axis, steps):
    count = lax.axis_size(axis)
    pairs = [(source, (source + steps) % count) for source in range(count)]
    return lax.ppermute(value, axis, pairs)


def over_axes(x, axes):
    for axis in axes:
        x = lax.psum(x, axis)
    return x


def fold_rows(weight, operand):
    return jnp.dot(operand, gathered_copies(weight, SUB, 0), preferred_element_type=jnp.float32)


def edge_rows(weight, operand):
    storage = jnp.zeros((1, weight.shape[1]), jnp.bfloat16)
    total = jnp.dot(operand, gather_axes(weight, SUB, 0), preferred_element_type=jnp.float32)
    return (total, storage)


def along_face(values, offset):
    return passed_along(values, FACE, offset)


def along_sub(values, offset):
    return passed_along(values, SUB, offset)


def per_device(
    mesh_latent,
    edge_latent,
    grid_features,
    senders,
    receivers,
    send_lists,
    link_sources,
    link_targets,
    node_area,
    grid_weight,
    encode_weight,
    edge_first,
    edge_second,
    node_first,
    node_second,
):
    node_rows = mesh_latent.shape[0]
    nodes_all = node_rows * lax.axis_size(FACE) * lax.axis_size(SUB)
    grid_latent = jax.nn.silu(
        jnp.dot(
            grid_features, gathered_copies(grid_weight, SUB, 1), preferred_element_type=jnp.float32
        )
    ).astype(jnp.bfloat16)

    def project(weight, operand):
        return fold_rows(weight, operand)

    node_ids = jnp.arange(node_rows, dtype=jnp.int32)
    joined = jnp.concatenate(
        [jnp.take(grid_latent, link_sources, axis=0), jnp.take(mesh_latent, link_targets, axis=0)],
        axis=1,
    )
    messages = jax.nn.silu(project(encode_weight, joined)).astype(jnp.bfloat16)
    target_onehot = (link_targets[:, None] == node_ids[None, :]).astype(jnp.bfloat16)
    arriving = lax.dot_general(
        target_onehot, messages, (((0,), (0,)), ((), ())), preferred_element_type=jnp.float32
    )
    latent = (mesh_latent.astype(jnp.float32) + arriving).astype(jnp.bfloat16)
    halo_lists = send_lists[0]
    list_mask = (halo_lists >= 0)[:, :, None]
    receive_onehot = (receivers[:, None] == node_ids[None, :]).astype(jnp.bfloat16)
    edge_state = edge_latent
    picked = jnp.take(latent, jnp.maximum(halo_lists, 0), axis=0)
    picked = jnp.where(list_mask, picked, jnp.zeros((), jnp.bfloat16))
    lower_face = along_face(picked[0], 1)
    upper_face = along_face(picked[1], -1)
    lower_sub = along_sub(picked[2], 1)
    upper_sub = along_sub(picked[3], -1)
    arrived = jnp.concatenate([lower_face, upper_face, lower_sub, upper_sub], axis=0)
    receiving_rows = jnp.take(latent, receivers, axis=0)
    node_table = jnp.concatenate([latent, arrived], axis=0)
    inputs = jnp.concatenate(
        [edge_state, jnp.take(node_table, senders, axis=0), receiving_rows], axis=1
    )
    before, unused_rows = edge_rows(edge_first[0], inputs)
    hidden = jax.nn.silu(before).astype(jnp.bfloat16)
    edge_state = (edge_state.astype(jnp.float32) + project(edge_second[0], hidden)).astype(
        jnp.bfloat16
    )
    incoming = lax.dot_general(
        receive_onehot, edge_state, (((0,), (0,)), ((), ())), preferred_element_type=jnp.float32
    ).astype(jnp.bfloat16)
    node_hidden = jax.nn.silu(
        project(node_first[0], jnp.concatenate([latent, incoming], axis=1))
    ).astype(jnp.bfloat16)
    latent = (latent.astype(jnp.float32) + project(node_second[0], node_hidden)).astype(
        jnp.bfloat16
    )
    totals = [jnp.dot(node_area, latent.astype(jnp.float32), precision=lax.Precision.HIGHEST)]
    stacked = over_axes(jnp.stack(totals), FACE_SUB)
    masses = stacked / nodes_all
    return (latent, edge_state, masses)


def solution(mesh):
    split = Mesh(mesh.devices.reshape(8, 2, 4, 4), ("face_0", "face_1", "sub_0", "sub_1"))
    placed = (
        P(FACE_SUB, None),
        P(FACE_SUB, None),
        P(FACE_SUB, None),
        P(FACE_SUB),
        P(FACE_SUB),
        P(FACE_SUB, None, None),
        P(FACE_SUB),
        P(FACE_SUB),
        P(FACE_SUB),
        P(None, SUB),
        P(SUB, None),
        P(None, SUB, None),
        P(None, SUB, None),
        P(None, SUB, None),
        P(None, SUB, None),
    )
    return jax.shard_map(
        per_device,
        mesh=split,
        in_specs=placed,
        out_specs=(P(FACE_SUB, None), P(FACE_SUB, None), P()),
        check_vma=False,
    )
```

profile of v0, /device:TPU:1, one launch (start us, length us, event | category | flops | bytes accessed | tf_op | source)
XLA Modules:
  0.0 170.4 jit_solution(7580788264351070964)
XLA Ops:
  7.2 0.0 copy-start
  7.2 0.0 copy-start.11
  7.2 0.0 copy-start.12
  7.2 0.0 copy-start.10
  7.2 0.0 copy-start.8
  7.2 0.0 copy-start.9
  7.2 1.6 broadcast_in_dim.73
  8.8 7.6 %all-to-all-start = ((bf16[16,384,32]{1,2,0:T(8,128)(2,1)}), bf16[16,384,32]{1,2,0:T(8,128)(2,1)S(1)}, u32[]{:S(2)}, u32[]{:S(2)}) async-start(bf16[16,384,32]{1,2,0:T(8,128)(2,1)} %broadcast_in_dim.73), calls=%async_computation | async-start | bytes 786432 | tf_op jit(solution)/shard_map/all_to_all | solution.py:20
  16.4 0.0 copy-start.1
  16.4 0.0 all-gather.4.cloned.1.call-start
  16.5 13.8 %all-gather = bf16[1,384,512]{2,1,0:T(8,128)(2,1)} all-gather(bf16[1,96,512]{2,1,0:T(8,128)(2,1)} %param.28), channel_id=2, replica_groups=mesh['face_0'=8,'face_1'=2,'sub_0'=4,'sub_1'=4] {'sub_1'}, dimensions={1}, use_global_device_ids=true | all-gather | bytes 491520 | tf_op jit(solution)/shard_map/all_gather | solution.py:29
  30.3 0.0 all-gather.4.cloned.1.call-update
  30.3 0.7 compare_select_fusion.2
  31.1 0.0 copy-done.9
  31.1 0.1 reshape.90
  31.2 0.0 all-to-all-done
  31.3 1.1 broadcast_in_dim.74
  32.3 5.0 %all-to-all-start.1 = ((bf16[16,64,512]{2,1,0:T(8,128)(2,1)}), bf16[16,64,512]{2,1,0:T(8,128)(2,1)S(1)}, u32[]{:S(2)}, u32[]{:S(2)}) async-start(bf16[16,64,512]{2,1,0:T(8,128)(2,1)} %broadcast_in_dim.74), calls=%async_computation.1 | async-start | bytes 2097152 | tf_op jit(solution)/shard_map/all_to_all | solution.py:20
  37.3 0.0 copy-done.1
  37.3 2.0 %gather_fusion.4 = bf16[512,512]{1,0:T(8,128)(2,1)S(1)} fusion(bf16[256,512]{1,0:T(8,128)(2,1)S(1)} %copy-done.1, s32[1024]{0:T(1024)S(1)} %get-tuple-element.13), kind=kCustom, calls=%fused_computation.1.clone | custom fusion | bytes 1050624 | tf_op jit(solution)/shard_map/jit(_take)/gather | solution.py:93
  39.3 0.1 broadcast_select_fusion.2
  39.5 0.4 multiply_convert_fusion.4
  39.9 0.0 copy-start.6
  39.9 2.0 %gather_fusion.3 = bf16[512,512]{1,0:T(8,128)(2,1)S(1)} fusion(bf16[256,512]{1,0:T(8,128)(2,1)S(1)} %multiply_convert_fusion.4, s32[1024]{0:T(1024)S(1)} %pad_clamp_fusion.2), kind=kCustom, calls=%fused_computation.clone | custom fusion | bytes 1050624 | tf_op jit(solution)/shard_map/jit(_take)/gather | solution.py:93
  41.9 0.1 broadcast_select_fusion.3
  42.0 9.0 %all-to-all-done.1 = bf16[16,64,512]{2,1,0:T(8,128)(2,1)S(1)} async-done(((bf16[16,64,512]{2,1,0:T(8,128)(2,1)}), bf16[16,64,512]{2,1,0:T(8,128)(2,1)S(1)}, u32[]{:S(2)}, u32[]{:S(2)}) %all-to-all-start.1) | async-done | bytes 1048608 | tf_op jit(solution)/shard_map/all_to_all | solution.py:20
  51.0 0.9 broadcast_in_dim.84
  51.9 4.2 %all-to-all-start.2 = ((bf16[16,32,512]{2,1,0:T(8,128)(2,1)}), bf16[16,32,512]{2,1,0:T(8,128)(2,1)}, u32[]{:S(2)}, u32[]{:S(2)}) async-start(bf16[16,32,512]{2,1,0:T(8,128)(2,1)} %broadcast_in_dim.84), calls=%async_computation.2 | async-start | bytes 1048576 | tf_op jit(solution)/shard_map/all_to_all | solution.py:20
  56.1 1.1 constant_dynamic-update-slice_fusion.4
  57.2 0.8 gather_fusion
  58.1 0.1 select_select_fusion
  58.2 6.5 %collective-permute-start = (bf16[32,512]{1,0:T(8,128)(2,1)S(1)}, bf16[32,512]{1,0:T(8,128)(2,1)S(1)}, u32[]{:S(2)}, u32[]{:S(2)}) collective-permute-start(bf16[32,512]{1,0:T(8,128)(2,1)S(1)} %get-tuple-element.7), channel_id=1, source_target_pairs={{0,16},{16,32},{32,48},{48,64},{64,80},{80,96},{96,112},{112,128},... | collective-permute-start | bytes 98312 | tf_op jit(solution)/shard_map/ppermute | solution.py:36
  64.7 0.0 collective-permute-start.1
  64.7 1.5 collective-permute-start.2
  66.2 3.4 %collective-permute-start.3 = (bf16[32,512]{1,0:T(8,128)(2,1)S(1)}, bf16[32,512]{1,0:T(8,128)(2,1)S(1)}, u32[]{:S(2)}, u32[]{:S(2)}) collective-permute-start(bf16[32,512]{1,0:T(8,128)(2,1)S(1)} %get-tuple-element.4), channel_id=1, source_target_pairs={{0,15},{1,0},{2,1},{3,2},{4,3},{5,4},{6,5},{7,6},{8,7},{9,8},{10,9... | collective-permute-start | bytes 98312 | tf_op jit(solution)/shard_map/ppermute | solution.py:36
  69.6 7.5 %gather_fusion.2 = bf16[2048,512]{1,0:T(8,128)(2,1)S(1)} fusion(bf16[256,512]{1,0:T(8,128)(2,1)S(1)} %get-tuple-element.11, s32[2048]{0:T(1024)S(1)} %fusion.40), kind=kCustom, calls=%fused_computation.4 | custom fusion | bytes 4202496 | tf_op jit(solution)/shard_map/jit(_take)/gather | solution.py:113
  77.1 1.5 broadcast_select_fusion
  78.7 0.0 collective-permute-done
  78.7 0.0 collective-permute-done.1
  78.7 0.0 collective-permute-done.2
  78.7 0.0 collective-permute-done.3
  78.8 0.0 copy-start.7
  78.8 7.5 %gather_fusion.1 = bf16[2048,512]{1,0:T(8,128)(2,1)S(1)} fusion(bf16[384,512]{1,0:T(8,128)(2,1)S(1)} %constant_dynamic-update-slice_fusion, s32[2048]{0:T(1024)S(1)} %fusion.39), kind=kCustom, calls=%fused_computation.3 | custom fusion | bytes 4202496 | tf_op jit(solution)/shard_map/jit(_take)/gather | solution.py:116
  86.3 0.0 all-to-all-done.2
  86.3 0.8 broadcast_in_dim.86
  87.2 4.2 %all-to-all-start.4 = ((bf16[16,32,512]{2,1,0:T(8,128)(2,1)}), bf16[16,32,512]{2,1,0:T(8,128)(2,1)}, u32[]{:S(2)}, u32[]{:S(2)}) async-start(bf16[16,32,512]{2,1,0:T(8,128)(2,1)} %broadcast_in_dim.86), calls=%async_computation.4 | async-start | bytes 1048576 | tf_op jit(solution)/shard_map/all_to_all | solution.py:20
  91.4 0.0 copy-start.5
  91.4 1.6 broadcast_select_fusion.1
  93.0 8.4 %all-to-all-done.4 = bf16[16,32,512]{2,1,0:T(8,128)(2,1)} async-done(((bf16[16,32,512]{2,1,0:T(8,128)(2,1)}), bf16[16,32,512]{2,1,0:T(8,128)(2,1)}, u32[]{:S(2)}, u32[]{:S(2)}) %all-to-all-start.4) | async-done | bytes 524320 | tf_op jit(solution)/shard_map/all_to_all | solution.py:20
  101.4 1.1 broadcast_in_dim.85
  102.4 4.3 %all-to-all-start.3 = ((bf16[16,64,512]{2,1,0:T(8,128)(2,1)}), bf16[16,64,512]{2,1,0:T(8,128)(2,1)}, u32[]{:S(2)}, u32[]{:S(2)}) async-start(bf16[16,64,512]{2,1,0:T(8,128)(2,1)} %broadcast_in_dim.85), calls=%async_computation.3 | async-start | bytes 2097152 | tf_op jit(solution)/shard_map/all_to_all | solution.py:20
  106.8 0.0 all-gather.4.cloned.1.call-done
  106.8 8.6 %add_convert_fusion = bf16[2048,512]{1,0:T(8,128)(2,1)} fusion(bf16[2048,512]{1,0:T(8,128)(2,1)} %param.18, bf16[512,512]{1,0:T(8,128)(2,1)} %bitcast.12, bf16[2048,512]{1,0:T(8,128)(2,1)S(1)} %copy-done.2, bf16[2048,512]{1,0:T(8,128)(2,1)} %broadcast_select_fusion.1, bf16[1,1536,512]{2,1,0:T(8,128)(2,1)} %all-gather.4.cloned.1.call-done), kind=kOutput, calls=%fused_computation.11 | convolution fusion | flops 4322230272 | bytes 10485760 | tf_op jit(solution)/shard_map/dot_general | solution.py:46
  115.5 2.7 %fusion.8 = bf16[256,512]{1,0:T(8,128)(2,1)S(1)} fusion(bf16[2048,512]{1,0:T(8,128)(2,1)} %add_convert_fusion, s32[2048]{0:T(1024)S(1)} %copy-done.9), kind=kOutput, calls=%fused_computation.20 | convolution fusion | flops 537526272 | bytes 2367488 | tf_op jit(solution)/shard_map/dot_general | solution.py:123
  118.2 3.5 %all-to-all-done.3 = bf16[16,64,512]{2,1,0:T(8,128)(2,1)} async-done(((bf16[16,64,512]{2,1,0:T(8,128)(2,1)}), bf16[16,64,512]{2,1,0:T(8,128)(2,1)}, u32[]{:S(2)}, u32[]{:S(2)}) %all-to-all-start.3) | async-done | bytes 1048608 | tf_op jit(solution)/shard_map/all_to_all | solution.py:20
  121.7 2.1 %fusion.10 = bf16[256,512]{1,0:T(8,128)(2,1)S(1)} fusion(bf16[512,512]{1,0:T(8,128)(2,1)} %bitcast.16, bf16[1024,512]{1,0:T(8,128)(2,1)} %bitcast.14, bf16[256,512]{1,0:T(8,128)(2,1)S(1)} %fusion.8, bf16[256,512]{1,0:T(8,128)(2,1)S(1)} %get-tuple-element.11), kind=kOutput, calls=%fused_computation.22 | convolution fusion | flops 404750336 | bytes 2359296 | tf_op jit(solution)/shard_map/dot_general | solution.py:46
  123.8 0.0 copy-start.3
  123.8 0.2 fusion.52
  124.0 18.4 %psum.28 = f32[1,512]{1,0:T(1,128)S(1)} all-reduce(f32[1,512]{1,0:T(1,128)S(1)} %fusion.52), channel_id=1, replica_groups=mesh['face_0'=8,'face_1'=2,'sub_0'=4,'sub_1'=4] {'face_0'}, use_global_device_ids=true, to_apply=%region_0.2 | all-reduce | flops 512 | bytes 4096 | tf_op jit(solution)/shard_map/psum | solution.py:41
  142.4 7.4 %psum.29 = f32[1,512]{1,0:T(1,128)S(1)} all-reduce(f32[1,512]{1,0:T(1,128)S(1)} %psum.28), channel_id=1, replica_groups=mesh['face_0'=8,'face_1'=2,'sub_0'=4,'sub_1'=4] {'face_1'}, use_global_device_ids=true, to_apply=%region_1.3 | all-reduce | flops 512 | bytes 4096 | tf_op jit(solution)/shard_map/psum | solution.py:41
  149.8 6.2 %psum.30 = f32[1,512]{1,0:T(1,128)S(1)} all-reduce(f32[1,512]{1,0:T(1,128)S(1)} %psum.29), channel_id=1, replica_groups=mesh['face_0'=8,'face_1'=2,'sub_0'=4,'sub_1'=4] {'sub_0'}, use_global_device_ids=true, to_apply=%region_2.4 | all-reduce | flops 512 | bytes 4096 | tf_op jit(solution)/shard_map/psum | solution.py:41
  156.0 6.9 %psum.31 = f32[1,512]{1,0:T(1,128)S(1)} all-reduce(f32[1,512]{1,0:T(1,128)S(1)} %psum.30), channel_id=1, replica_groups=mesh['face_0'=8,'face_1'=2,'sub_0'=4,'sub_1'=4] {'sub_1'}, use_global_device_ids=true, to_apply=%region_3.5 | all-reduce | flops 512 | bytes 4096 | tf_op jit(solution)/shard_map/psum | solution.py:41
  163.0 0.6 broadcast_multiply_fusion
  163.6 0.0 copy-done.3
  (30 shorter events, 0.1 us)
Async XLA Ops:
  7.2 32.3 %copy-start = (bf16[256,384]{1,0:T(8,128)(2,1)S(1)}, bf16[256,384]{1,0:T(8,128)(2,1)}, u32[]{:S(2)}) copy-start(bf16[256,384]{1,0:T(8,128)(2,1)} %param.19) | copy-start | bytes 589828
  7.2 23.8 %copy-start.11 = (s32[512]{0:T(512)S(1)}, s32[512]{0:T(512)}, u32[]{:S(2)}) copy-start(s32[512]{0:T(512)} %param.24) | copy-start | bytes 6148
  7.2 23.8 %copy-start.12 = (s32[1,4,32]{2,1,0:T(4,128)S(1)}, s32[1,4,32]{2,1,0:T(4,128)}, u32[]{:S(2)}) copy-start(s32[1,4,32]{2,1,0:T(4,128)} %param.22) | copy-start | bytes 1540
  7.2 23.9 %copy-start.10 = (s32[512]{0:T(512)S(1)}, s32[512]{0:T(512)}, u32[]{:S(2)}) copy-start(s32[512]{0:T(512)} %param.23) | copy-start | bytes 6148
  7.2 23.9 %copy-start.8 = (s32[2048]{0:T(1024)S(1)}, s32[2048]{0:T(1024)}, u32[]{:S(2)}) copy-start(s32[2048]{0:T(1024)} %param.20) | copy-start | bytes 24580
  7.2 23.9 %copy-start.9 = (s32[2048]{0:T(1024)S(1)}, s32[2048]{0:T(1024)}, u32[]{:S(2)}) copy-start(s32[2048]{0:T(1024)} %param.21) | copy-start | bytes 24580
  7.2 24.0 %copy-start.4 = (bf16[64,512]{1,0:T(8,128)(2,1)S(1)}, bf16[64,512]{1,0:T(8,128)(2,1)}, u32[]{:S(2)}) copy-start(bf16[64,512]{1,0:T(8,128)(2,1)} %param.27) | copy-start | bytes 196612
  8.8 22.4 %all-to-all-start = ((bf16[16,384,32]{1,2,0:T(8,128)(2,1)}), bf16[16,384,32]{1,2,0:T(8,128)(2,1)S(1)}, u32[]{:S(2)}, u32[]{:S(2)}) async-start(bf16[16,384,32]{1,2,0:T(8,128)(2,1)} %broadcast_in_dim.73), calls=%async_computation | async-start | bytes 786432 | tf_op jit(solution)/shard_map/all_to_all | solution.py:20
  16.4 20.9 %copy-start.1 = (bf16[256,512]{1,0:T(8,128)(2,1)S(1)}, bf16[256,512]{1,0:T(8,128)(2,1)}, u32[]{:S(2)}) copy-start(bf16[256,512]{1,0:T(8,128)(2,1)} %param.17) | copy-start | bytes 786436
  16.4 90.4 %all-gather.4.cloned.1.call-start = ((), (), s32[]{:S(2)}) async-start(), calls=%async_computation.5 | async-start | bytes 1966080 | tf_op jit(solution)/shard_map/all_gather | solution.py:29
  32.3 18.7 %all-to-all-start.1 = ((bf16[16,64,512]{2,1,0:T(8,128)(2,1)}), bf16[16,64,512]{2,1,0:T(8,128)(2,1)S(1)}, u32[]{:S(2)}, u32[]{:S(2)}) async-start(bf16[16,64,512]{2,1,0:T(8,128)(2,1)} %broadcast_in_dim.74), calls=%async_computation.1 | async-start | bytes 2097152 | tf_op jit(solution)/shard_map/all_to_all | solution.py:20
  39.9 11.1 %copy-start.6 = (bf16[1,32,512]{2,1,0:T(8,128)(2,1)S(1)}, bf16[1,32,512]{2,1,0:T(8,128)(2,1)}, u32[]{:S(2)}) copy-start(bf16[1,32,512]{2,1,0:T(8,128)(2,1)} %param.29) | copy-start | bytes 98308
  51.9 34.5 %all-to-all-start.2 = ((bf16[16,32,512]{2,1,0:T(8,128)(2,1)}), bf16[16,32,512]{2,1,0:T(8,128)(2,1)}, u32[]{:S(2)}, u32[]{:S(2)}) async-start(bf16[16,32,512]{2,1,0:T(8,128)(2,1)} %broadcast_in_dim.84), calls=%async_computation.2 | async-start | bytes 1048576 | tf_op jit(solution)/shard_map/all_to_all | solution.py:20
  58.2 20.5 %collective-permute-start = (bf16[32,512]{1,0:T(8,128)(2,1)S(1)}, bf16[32,512]{1,0:T(8,128)(2,1)S(1)}, u32[]{:S(2)}, u32[]{:S(2)}) collective-permute-start(bf16[32,512]{1,0:T(8,128)(2,1)S(1)} %get-tuple-element.7), channel_id=1, source_target_pairs={{0,16},{16,32},{32,48},{48,64},{64,80},{80,96},{96,112},{112,128},... | collective-permute-start | bytes 98312 | tf_op jit(solution)/shard_map/ppermute | solution.py:36
  64.7 14.0 %collective-permute-start.1 = (bf16[32,512]{1,0:T(8,128)(2,1)S(1)}, bf16[32,512]{1,0:T(8,128)(2,1)S(1)}, u32[]{:S(2)}, u32[]{:S(2)}) collective-permute-start(bf16[32,512]{1,0:T(8,128)(2,1)S(1)} %get-tuple-element.6), channel_id=1, source_target_pairs={{0,240},{16,0},{32,16},{48,32},{64,48},{80,64},{96,80},{112,96},{1... | collective-permute-start | bytes 98312 | tf_op jit(solution)/shard_map/ppermute | solution.py:36
  64.7 14.0 %collective-permute-start.2 = (bf16[32,512]{1,0:T(8,128)(2,1)S(1)}, bf16[32,512]{1,0:T(8,128)(2,1)S(1)}, u32[]{:S(2)}, u32[]{:S(2)}) collective-permute-start(bf16[32,512]{1,0:T(8,128)(2,1)S(1)} %get-tuple-element.5), channel_id=1, source_target_pairs={{0,1},{1,2},{2,3},{3,4},{4,5},{5,6},{6,7},{7,8},{8,9},{9,10},{10,1... | collective-permute-start | bytes 98312 | tf_op jit(solution)/shard_map/ppermute | solution.py:36
  66.2 12.6 %collective-permute-start.3 = (bf16[32,512]{1,0:T(8,128)(2,1)S(1)}, bf16[32,512]{1,0:T(8,128)(2,1)S(1)}, u32[]{:S(2)}, u32[]{:S(2)}) collective-permute-start(bf16[32,512]{1,0:T(8,128)(2,1)S(1)} %get-tuple-element.4), channel_id=1, source_target_pairs={{0,15},{1,0},{2,1},{3,2},{4,3},{5,4},{6,5},{7,6},{8,7},{9,8},{10,9... | collective-permute-start | bytes 98312 | tf_op jit(solution)/shard_map/ppermute | solution.py:36
  78.8 7.6 %copy-start.7 = (bf16[1,32,512]{2,1,0:T(8,128)(2,1)S(1)}, bf16[1,32,512]{2,1,0:T(8,128)(2,1)}, u32[]{:S(2)}) copy-start(bf16[1,32,512]{2,1,0:T(8,128)(2,1)} %param.31) | copy-start | bytes 98308
  87.2 14.2 %all-to-all-start.4 = ((bf16[16,32,512]{2,1,0:T(8,128)(2,1)}), bf16[16,32,512]{2,1,0:T(8,128)(2,1)}, u32[]{:S(2)}, u32[]{:S(2)}) async-start(bf16[16,32,512]{2,1,0:T(8,128)(2,1)} %broadcast_in_dim.86), calls=%async_computation.4 | async-start | bytes 1048576 | tf_op jit(solution)/shard_map/all_to_all | solution.py:20
  91.4 9.9 %copy-start.5 = (bf16[1,64,512]{2,1,0:T(8,128)(2,1)S(1)}, bf16[1,64,512]{2,1,0:T(8,128)(2,1)}, u32[]{:S(2)}) copy-start(bf16[1,64,512]{2,1,0:T(8,128)(2,1)} %param.30) | copy-start | bytes 196612
  93.0 13.8 %copy-start.2 = (bf16[2048,512]{1,0:T(8,128)(2,1)S(1)}, bf16[2048,512]{1,0:T(8,128)(2,1)}, u32[]{:S(2)}) copy-start(bf16[2048,512]{1,0:T(8,128)(2,1)} %broadcast_select_fusion) | copy-start | bytes 6291460
  102.4 19.2 %all-to-all-start.3 = ((bf16[16,64,512]{2,1,0:T(8,128)(2,1)}), bf16[16,64,512]{2,1,0:T(8,128)(2,1)}, u32[]{:S(2)}, u32[]{:S(2)}) async-start(bf16[16,64,512]{2,1,0:T(8,128)(2,1)} %broadcast_in_dim.85), calls=%async_computation.3 | async-start | bytes 2097152 | tf_op jit(solution)/shard_map/all_to_all | solution.py:20
  121.7 2.1 %copy-start.13 = (f32[256]{0:T(256)S(1)}, f32[256]{0:T(256)}, u32[]{:S(2)}) copy-start(f32[256]{0:T(256)} %param.25) | copy-start | bytes 3076
  123.8 39.8 %copy-start.3 = (bf16[256,512]{1,0:T(8,128)(2,1)}, bf16[256,512]{1,0:T(8,128)(2,1)S(1)}, u32[]{:S(2)}) copy-start(bf16[256,512]{1,0:T(8,128)(2,1)S(1)} %fusion.10) | copy-start | bytes 786436
Sparse Core Ops, SparseCore 0:
  30.4 41.9 all-gather.3
where the time goes:
time: 173 us; the launch traced here: 170 us
  blocking collectives  52.8 us (31%)
  starting transfers between devices  36.8 us (21%)
  local copies, waits for them, and re-layouts  25.5 us (15%)
  waiting for transfers between devices  20.9 us (12%)
  matrix products  15.1 us (9%)
  between operations  14.5 us (8%)
  other arithmetic  4.81 us (3%)
    psum x4, blocking collectives, over_axes(): x = lax.psum(x, axis)  39 us
    all_to_all x5, starting transfers between devices, from_everyone(): return lax.all_to_all(copies, axis, split_axis=0, concat_axis=0, tiled=True)  25.3 us
    all_to_all x5, waiting for transfers between devices, from_everyone(): return lax.all_to_all(copies, axis, split_axis=0, concat_axis=0, tiled=True)  20.9 us
    all_gather x1, blocking collectives, gather_axes(): x = lax.all_gather(x, axis, axis=dim, tiled=True)  13.8 us
    ppermute x4, starting transfers between devices, passed_along(): return lax.ppermute(value, axis, pairs)  11.4 us
    dot_general x2, matrix products, fold_rows(): jnp.dot(operand, gathered_copies(weight, SUB, 0), preferred_element_type=...  10.7 us
    gather x1, local copies, waits for them, and re-layouts, per_device(): jnp.take(node_table, senders, axis=0)  7.54 us
    gather x1, local copies, waits for them, and re-layouts, per_device(): receiving_rows = jnp.take(latent, receivers, axis=0)  7.53 us
  transfers between devices with their start and end apart: 10, of which 3 were waited for; matrix products, arithmetic and copies ran while one was open for 24% of the time, Pallas kernels for 0%

commit v1 on v0

v1 whole, which is shorter than its diff:
```python
import functools

import jax
import jax.numpy as jnp
from jax import lax
from jax.experimental import pallas as pl
from jax.experimental.pallas import tpu as pltpu
from jax.sharding import PartitionSpec as P

BF = jnp.bfloat16
F32 = jnp.float32
MESH = pl.DeviceIdType.MESH

GRID_AT, ENC_AT, EF_AT, ES_AT, NF_AT, NS_AT, ROWS = 0, 16, 48, 96, 112, 144, 160
GROUPS = ((0, 48), (48, 96), (96, 160))
TILE = 512


def silu(v):
    h = 0.5 * v
    return h + h * jnp.tanh(h)


def dot(a, b):
    return jnp.dot(a, b, preferred_element_type=F32)


def column(row):
    return jnp.broadcast_to(row, (128, 128)).T


def kernel(
    mesh_h, edge_h, gridf_h, snd_h, rcv_h, lists_h, lsrc_h, ltgt_h, area_h,
    gw_h, enc_h, ef_h, es_h, nf_h, ns_h,
    mesh_o, edge_o, mass_o,
    buf, gs, mesh_v, gridf_v, x_v, snd_v, rcv_v, lists_v, lsrc_v, ltgt_v, area_v,
    gt_w, enc_w, r_w, w23, es_w, nf_w, ns_w,
    ol, olt, ort, e1, new_v, l0, res_v, hs, hr, acol, msrc, asub, fsrc, aface,
    in_sem, w_sem, out_sem,
    p1_s, p1_r, p1f_s, p1f_r, p2_s, p2_r, p2f_s, p2f_r, dd_s, dd_r,
    h_s, h_r, ms_s, ms_r, mf_s, mf_r,
):
    f = lax.axis_index("face")
    s = lax.axis_index("sub")
    c = lax.rem(f, 2)
    y, x = lax.div(s, 4), lax.rem(s, 4)
    b = y + c * (x - y)
    a = x + c * (y - x)
    wa, wb = 1 + 3 * c, 4 - 3 * c
    a_r, a_l, a_2 = lax.rem(a + 1, 4), lax.rem(a + 3, 4), lax.rem(a + 2, 4)
    b_r, b_l, b_2 = lax.rem(b + 1, 4), lax.rem(b + 3, 4), lax.rem(b + 2, 4)
    to_ar, to_al = (f, b * wb + a_r * wa), (f, b * wb + a_l * wa)
    to_br, to_bl = (f, b_r * wb + a * wa), (f, b_l * wb + a * wa)
    sibling = (f + 1 - 2 * c, s)
    other = 1 - c

    loads = []
    for at, rows, ref in (
        (ENC_AT, 32, enc_h), (EF_AT, 48, ef_h), (ES_AT, 16, es_h), (NF_AT, 32, nf_h), (NS_AT, 16, ns_h),
    ):
        n = len(loads)
        loads.append(pltpu.make_async_copy(
            ref.at[pl.ds(c * rows, rows)], buf.at[c, b, a, pl.ds(at, rows)], w_sem.at[n]))
        loads.append(pltpu.make_async_copy(
            ref.at[pl.ds(other * rows, rows)], buf.at[other, a, b, pl.ds(at, rows)], w_sem.at[n + 1]))
    gload = pltpu.make_async_copy(gw_h, gs, w_sem.at[10])
    gload.start()
    for copy in loads:
        copy.start()
    ins = [
        pltpu.make_async_copy(src, dst, in_sem.at[n])
        for n, (src, dst) in enumerate((
            (lsrc_h, lsrc_v), (ltgt_h, ltgt_v), (snd_h, snd_v), (rcv_h, rcv_v), (lists_h, lists_v),
            (area_h, area_v), (gridf_h, gridf_v), (mesh_h, mesh_v), (edge_h, x_v.at[:, pl.ds(0, 512)]),
        ))
    ]
    for copy in ins:
        copy.start()

    barrier = pltpu.get_barrier_semaphore()
    for k in range(1, 16):
        pl.semaphore_signal(barrier, inc=1, device_id=(f, lax.rem(s + k, 16)), device_id_type=MESH)
        pl.semaphore_signal(barrier, inc=1, device_id=(lax.rem(f + k, 16), s), device_id_type=MESH)

    gload.wait()
    turned = gs[...].astype(F32).T.astype(BF)
    first, second = turned[0:16], turned[16:32]
    mine = jnp.where(c == 0, first, second)
    theirs = jnp.where(c == 0, second, first)
    pad = jnp.zeros((16, 128), BF)
    buf[c, b, a, 0:16, :] = jnp.concatenate([mine, pad], axis=1)
    buf[other, a, b, 0:16, :] = jnp.concatenate([theirs, pad], axis=1)
    for copy in loads:
        copy.wait()

    pl.semaphore_wait(barrier, 30)

    def remote(src, dst, send, recv, to):
        copy = pltpu.make_async_remote_copy(
            src_ref=src, dst_ref=dst, send_sem=send, recv_sem=recv, device_id=to, device_id_type=MESH)
        return copy

    def same(ref, send, recv, to):
        return remote(ref, ref, send, recv, to)

    p1, p1f, p2, p2f, dd = [], [], [], [], []
    for g, (lo, hi) in enumerate(GROUPS):
        rows = pl.ds(lo, hi - lo)
        p1.append([
            same(buf.at[c, b, a, rows], p1_s.at[g, 0], p1_r.at[g, 0], to_ar),
            same(buf.at[c, b, a, rows], p1_s.at[g, 1], p1_r.at[g, 1], to_al),
        ])
        left, right = pl.ds(0, 256), pl.ds(256, 256)
        p1f.append([
            same(buf.at[c, b, a_l, rows, left], p1f_s.at[g, 0], p1f_r.at[g, 0], to_ar),
            same(buf.at[c, b, a_r, rows, right], p1f_s.at[g, 1], p1f_r.at[g, 1], to_al),
        ])
        every = pl.ds(0, 4)
        p2.append([
            same(buf.at[c, b, every, rows], p2_s.at[g, 0], p2_r.at[g, 0], to_br),
            same(buf.at[c, b, every, rows], p2_s.at[g, 1], p2_r.at[g, 1], to_bl),
        ])
        p2f.append([
            same(buf.at[c, b_l, pl.ds(0, 2), rows], p2f_s.at[g, 0], p2f_r.at[g, 0], to_br),
            same(buf.at[c, b_r, pl.ds(2, 2), rows], p2f_s.at[g, 1], p2f_r.at[g, 1], to_bl),
        ])
        dd.append([
            same(buf.at[c, b, a_l, rows], dd_s.at[g, 0], dd_r.at[g, 0], sibling),
            same(buf.at[c, b, a_r, rows], dd_s.at[g, 1], dd_r.at[g, 1], sibling),
            same(buf.at[c, b, a_2, rows], dd_s.at[g, 2], dd_r.at[g, 2], sibling),
            same(buf.at[c, b_l, every, rows], dd_s.at[g, 3], dd_r.at[g, 3], sibling),
            same(buf.at[c, b_r, every, rows], dd_s.at[g, 4], dd_r.at[g, 4], sibling),
            same(buf.at[c, b_2, every, rows], dd_s.at[g, 5], dd_r.at[g, 5], sibling),
        ])

    def start(copies):
        for copy in copies:
            copy.start()

    def arrived(copies):
        for copy in copies:
            copy.wait_recv()

    def pass_p1(g):
        arrived(p1[g])
        start(p1f[g])
        start(dd[g][0:2])

    def pass_p1f(g):
        arrived(p1f[g])
        start(p2[g])
        start(dd[g][2:3])

    def pass_p2(g):
        arrived(p2[g])
        start(p2f[g])
        start(dd[g][3:5])

    def pass_p2f(g):
        arrived(p2f[g])
        start(dd[g][5:6])

    for g in range(3):
        start(p1[g])

    for copy in ins[0:6]:
        copy.wait()
    lanes = lax.broadcasted_iota(jnp.int32, (128, 128), 1).astype(F32)
    node_rows = lax.broadcasted_iota(jnp.int32, (256, 128), 0).astype(F32)

    def hot(col, first):
        return jnp.where(col == lanes + float(first), 1.0, 0.0).astype(BF)

    pass_p1(0)
    pass_p1(1)
    pass_p1(2)
    lsrc = lsrc_v[...].astype(F32)
    ltgt = ltgt_v[...].astype(F32)
    for j in range(4):
        col = column(lsrc[j:j + 1])
        for k in range(2):
            ol[128 * j:128 * (j + 1), 128 * k:128 * (k + 1)] = hot(col, 128 * k)
        col = column(ltgt[j:j + 1])
        for k in range(2):
            ol[128 * j:128 * (j + 1), 256 + 128 * k:256 + 128 * (k + 1)] = hot(col, 128 * k)
        olt[:, 128 * j:128 * (j + 1)] = jnp.where(node_rows == ltgt[j:j + 1], 1.0, 0.0).astype(BF)
    pass_p1f(0)
    pass_p1f(1)

    snd = snd_v[...].astype(F32)
    rcv = rcv_v[...].astype(F32)

    def edge_hot(js):
        for j in js:
            at = slice(128 * j, 128 * (j + 1))
            col = column(snd[j:j + 1])
            for k in range(2):
                x_v[at, 512 + 128 * k:512 + 128 * (k + 1)] = hot(col, 128 * k)
            x_v[at, 1024:1152] = hot(col, 256)
            col = column(rcv[j:j + 1])
            for k in range(2):
                x_v[at, 768 + 128 * k:768 + 128 * (k + 1)] = hot(col, 128 * k)
            t, o = j // 4, 128 * (j % 4)
            ort[t, :, o:o + 128] = jnp.where(node_rows == rcv[j:j + 1], 1.0, 0.0).astype(BF)

    edge_hot(range(0, 8))
    for j in range(2):
        acol[128 * j:128 * (j + 1), :] = column(area_v[j:j + 1, :])
    pass_p2(0)
    pass_p1f(2)
    edge_hot(range(8, 16))
    pass_p2f(0)
    pass_p2(1)

    def assemble(at, rows, put):
        for i in range(16):
            put(i * 2 * rows, buf[0, i // 4, i % 4, at:at + rows, :])
            put(i * 2 * rows + rows, buf[1, i % 4, i // 4, at:at + rows, :])

    arrived(dd[0])
    for i in range(16):
        gt_w[i * 32:i * 32 + 16, :] = buf[0, i // 4, i % 4, 0:16, 0:384]
        gt_w[i * 32 + 16:i * 32 + 32, :] = buf[1, i % 4, i // 4, 0:16, 0:384]

    def put_enc(at, block):
        enc_w[at:at + block.shape[0], :] = block

    assemble(ENC_AT, 32, put_enc)
    for copy in ins[6:9]:
        copy.wait()

    grid_latent = silu(lax.dot_general(
        gridf_v[...], gt_w[...], (((1,), (1,)), ((), ())), preferred_element_type=F32)).astype(BF)
    from_grid = dot(grid_latent, enc_w[0:512, :]).astype(BF)
    from_mesh = dot(mesh_v[...], enc_w[512:1024, :]).astype(BF)
    messages = silu(dot(ol[...], jnp.concatenate([from_grid, from_mesh], axis=0))).astype(BF)
    l0[...] = (mesh_v[...].astype(F32) + dot(olt[...], messages)).astype(BF)

    slot_rows = lax.broadcasted_iota(jnp.int32, (256, 32), 0)
    for d in range(4):
        pick = jnp.where(slot_rows == lists_v[d:d + 1, :], 1.0, 0.0).astype(BF)
        hs[d] = lax.dot_general(
            pick, l0[...], (((0,), (0,)), ((), ())), preferred_element_type=F32).astype(BF)
    targets = (
        (lax.rem(f + 1, 16), s), (lax.rem(f + 15, 16), s), (f, lax.rem(s + 1, 16)), (f, lax.rem(s + 15, 16)))
    halo = [remote(hs.at[d], hr.at[d], h_s.at[d], h_r.at[d], targets[d]) for d in range(4)]
    start(halo)
    pass_p2f(1)
    pass_p2(2)
    arrived(dd[1])

    def put_ef(at, block):
        done = 0
        while done < block.shape[0]:
            place = at + done
            limit = block.shape[0] - done if place >= 512 else min(block.shape[0] - done, 512 - place)
            if place < 512:
                r_w[place:place + limit, :] = block[done:done + limit]
            else:
                w23[place - 512:place - 512 + limit, :] = block[done:done + limit]
            done += limit

    assemble(EF_AT, 48, put_ef)
    r_w[512:768, :] = dot(l0[...], w23[0:512, :]).astype(BF)
    r_w[768:1024, :] = dot(l0[...], w23[512:1024, :]).astype(BF)
    for t in range(4):
        at = slice(TILE * t, TILE * (t + 1))
        e1[at, :] = dot(x_v[at, 0:1024], r_w[0:1024, :])
        if t == 1:
            pass_p2f(2)
    arrived(halo)
    r_w[1024:1152, :] = dot(hr[...].reshape(128, 512), w23[0:512, :]).astype(BF)
    arrived(dd[2])

    def put_to(ref):
        def put(at, block):
            ref[at:at + block.shape[0], :] = block
        return put

    assemble(ES_AT, 16, put_to(es_w))

    writes = []
    incoming = jnp.zeros((256, 512), F32)
    for t in range(4):
        at = slice(TILE * t, TILE * (t + 1))
        hidden = silu(e1[at, :] + dot(x_v[at, 1024:1152], r_w[1024:1152, :])).astype(BF)
        new = (x_v[at, 0:512].astype(F32) + dot(hidden, es_w[...])).astype(BF)
        new_v[at, :] = new
        write = pltpu.make_async_copy(new_v.at[pl.ds(TILE * t, TILE)], edge_o.at[pl.ds(TILE * t, TILE)], out_sem.at[t])
        write.start()
        writes.append(write)
        incoming = incoming + dot(ort[t], new)
    assemble(NF_AT, 32, put_to(nf_w))
    assemble(NS_AT, 16, put_to(ns_w))

    node_hidden = silu(dot(l0[...], nf_w[0:512, :]) + dot(incoming.astype(BF), nf_w[512:1024, :])).astype(BF)
    result = (l0[...].astype(F32) + dot(node_hidden, ns_w[...])).astype(BF)
    res_v[...] = result
    write = pltpu.make_async_copy(res_v, mesh_o, out_sem.at[4])
    write.start()
    writes.append(write)

    wide = result.astype(F32)
    msrc[...] = jnp.zeros((8, 128), F32)
    for k in range(4):
        msrc[k:k + 1, :] = jnp.sum(wide[:, 128 * k:128 * (k + 1)] * acol[...], axis=0, keepdims=True)

    def exchange(source, slots, me, peer, sends, recvs):
        slots[me] = source[...]
        copies = [
            remote(source, slots.at[me], sends.at[k - 1], recvs.at[me], peer(lax.rem(me + k, 16)))
            for k in range(1, 16)
        ]
        start(copies)
        for k in range(1, 16):
            j = lax.rem(me + k, 16)
            remote(source, slots.at[j], sends.at[k - 1], recvs.at[j], peer(j)).wait_recv()
        return copies

    by_sub = exchange(msrc, asub, s, lambda j: (f, j), ms_s, ms_r)
    fsrc[...] = jnp.sum(asub[...], axis=0)
    by_face = exchange(fsrc, aface, f, lambda j: (j, s), mf_s, mf_r)
    total = jnp.sum(aface[...], axis=0) / 65536.0
    for k in range(4):
        mass_o[0:1, 128 * k:128 * (k + 1)] = total[k:k + 1, :]

    for copy in writes:
        copy.wait()
    for group in p1 + p1f + p2 + p2f + dd + [halo, by_sub, by_face]:
        for copy in group:
            copy.wait_send()


def per_device(
    mesh_latent, edge_latent, grid_features, senders, receivers, send_lists, link_sources, link_targets,
    node_area, grid_weight, encode_weight, edge_first, edge_second, node_first, node_second,
):
    dma = pltpu.SemaphoreType.DMA
    vm = pltpu.VMEM
    return pl.pallas_call(
        kernel,
        out_shape=(
            jax.ShapeDtypeStruct((256, 512), BF),
            jax.ShapeDtypeStruct((2048, 512), BF),
            jax.ShapeDtypeStruct((1, 512), F32),
        ),
        in_specs=[pl.BlockSpec(memory_space=pl.ANY)] * 15,
        out_specs=(
            pl.BlockSpec(memory_space=pl.ANY),
            pl.BlockSpec(memory_space=pl.ANY),
            pl.BlockSpec(memory_space=pltpu.VMEM),
        ),
        scratch_shapes=[
            vm((2, 4, 4, ROWS, 512), BF), vm((384, 32), BF), vm((256, 512), BF), vm((256, 384), BF),
            vm((2048, 1152), BF), vm((16, 128), jnp.int32), vm((16, 128), jnp.int32), vm((4, 32), jnp.int32),
            vm((4, 128), jnp.int32), vm((4, 128), jnp.int32), vm((2, 128), F32),
            vm((512, 384), BF), vm((1024, 512), BF), vm((1152, 512), BF), vm((1024, 512), BF),
            vm((512, 512), BF), vm((1024, 512), BF), vm((512, 512), BF),
            vm((512, 512), BF), vm((256, 512), BF), vm((4, 256, 512), BF), vm((2048, 512), F32),
            vm((2048, 512), BF), vm((256, 512), BF), vm((256, 512), BF), vm((4, 32, 512), BF),
            vm((4, 32, 512), BF), vm((256, 128), F32), vm((8, 128), F32), vm((16, 8, 128), F32),
            vm((8, 128), F32), vm((16, 8, 128), F32),
            dma((9,)), dma((11,)), dma((5,)),
            dma((3, 2)), dma((3, 2)), dma((3, 2)), dma((3, 2)), dma((3, 2)), dma((3, 2)), dma((3, 2)), dma((3, 2)),
            dma((3, 6)), dma((3, 6)), dma((4,)), dma((4,)),
            dma((15,)), dma((16,)), dma((15,)), dma((16,)),
        ],
        compiler_params=pltpu.CompilerParams(
            collective_id=0, has_side_effects=True, vmem_limit_bytes=60 * 1024 * 1024),
        cost_estimate=pl.CostEstimate(flops=6_000_000_000, bytes_accessed=6_000_000, transcendentals=1_500_000),
        name="graph_layer",
    )(
        mesh_latent, edge_latent, grid_features, senders.reshape(16, 128), receivers.reshape(16, 128),
        send_lists[0], link_sources.reshape(4, 128), link_targets.reshape(4, 128), node_area.reshape(2, 128),
        grid_weight, encode_weight, edge_first[0], edge_second[0], node_first[0], node_second[0],
    )


def solution(mesh):
    both = ("face", "sub")
    placed = (
        P(both, None), P(both, None), P(both, None), P(both), P(both), P(both, None, None), P(both), P(both), P(both),
        P(None, "sub"), P("sub", None), P(None, "sub", None), P(None, "sub", None), P(None, "sub", None),
        P(None, "sub", None),
    )
    return jax.shard_map(
        per_device, mesh=mesh, in_specs=placed, out_specs=(P(both, None), P(both, None), P()), check_vma=False)
```

time: 173 us -> 60.5 us (0.35); the launches traced: 170 us -> 60.2 us
  Pallas kernels: 0 us -> 52.8 us
  blocking collectives: 52.8 us -> 0 us
  starting transfers between devices: 36.8 us -> 0 us
  waiting for transfers between devices: 20.9 us -> 0 us
  local copies, waits for them, and re-layouts: 25.5 us -> 6.78 us
  matrix products: 15.1 us -> 0 us
  between operations: 14.5 us -> 0.64 us
  other arithmetic: 4.81 us -> 0 us
    pallas_call x0 -> x1, Pallas kernels: none -> 52.8 us  [per_device(): pl.pallas_call(kernel, out_shape=(jax.ShapeDtypeStruct((256, 512), BF), j...]
    psum x4 -> x0, blocking collectives: 39 us -> none  [over_axes(): x = lax.psum(x, axis)]
    all_to_all x5 -> x0, starting transfers between devices: 25.3 us -> none  [from_everyone(): return lax.all_to_all(copies, axis, split_axis=0, concat_axis=0, tiled=True)]
    all_to_all x5 -> x0, waiting for transfers between devices: 20.9 us -> none  [from_everyone(): return lax.all_to_all(copies, axis, split_axis=0, concat_axis=0, tiled=True)]
    gather x5 -> x0, local copies, waits for them, and re-layouts: 19.9 us -> none  [the longest x1 7.54 us: per_device(): jnp.take(node_table, senders, axis=0)]
    dot_general x6 -> x0, matrix products: 15.1 us -> none  [the longest x2 10.7 us: fold_rows(): jnp.dot(operand, gathered_copies(weight, SUB, 0), preferred_element_type=...]
    all_gather x1 -> x0, blocking collectives: 13.8 us -> none  [gather_axes(): x = lax.all_gather(x, axis, axis=dim, tiled=True)]
    ppermute x4 -> x0, starting transfers between devices: 11.4 us -> none  [passed_along(): return lax.ppermute(value, axis, pairs)]
  transfers between devices with their start and end apart: 10 -> 0, of which waited for: 3 -> 0; matrix products, arithmetic and copies ran while one was open for 24% -> 0% of each run, Pallas kernels for 0% -> 0%
where the time goes in v1:
time: 60.5 us; the launch traced here: 60.2 us
  Pallas kernels  52.8 us (87%)
  local copies, waits for them, and re-layouts  6.78 us (11%)
  between operations  0.64 us (1%)
    pallas_call x1, Pallas kernels, per_device(): pl.pallas_call(kernel, out_shape=(jax.ShapeDtypeStruct((256, 512), BF), j...  52.8 us
    unnamed x6, local copies, waits for them, and re-layouts  6.78 us

profile of v1, /device:TPU:1, one launch (start us, length us, event | category | flops | bytes accessed | tf_op | source)
XLA Modules:
  0.0 60.2 jit_solution(2737600656339372920)
XLA Ops:
  0.6 1.5 %copy.18.gw_h = bf16[384,32]{1,0:T(8,128)(2,1)} copy(bf16[384,32]{0,1:T(8,128)(2,1)} %param.24) | data formatting | bytes 49152 | tf_op args[9]
  2.1 52.8 %graph_layer.1 = (bf16[256,512]{1,0:T(8,128)(2,1)}, bf16[2048,512]{1,0:T(8,128)(2,1)}, f32[1,512]{1,0:T(1,128)}) custom-call(bf16[256,512]{1,0:T(8,128)(2,1)} %mesh_h.1, bf16[2048,512]{1,0:T(8,128)(2,1)} %edge_h.1, bf16[256,384]{1,0:T(8,128)(2,1)} %gridf_h.1, s32[16,128]{1,0:T(8,128)} %bitcast.14, s32[16,128]{1,0:T(8,128)} %bitcast.15, s32[4,32]{1,0:T(4,128)} %bitcast.16, ...), custom_call_target="tpu_custom_call" | custom-call | flops 6000000000 | bytes 6000000 | tf_op jit(solution)/shard_map/graph_layer/pallas_call | solution.py:340
  54.9 1.7 %copy.22 = bf16[256,512]{1,0:T(8,128)(2,1)} copy(bf16[256,512]{1,0:T(8,128)(2,1)} %get-tuple-element.6) | data formatting | bytes 524288
  56.6 0.0 copy-start
  56.6 3.0 %copy.23 = bf16[2048,512]{1,0:T(8,128)(2,1)} copy(bf16[2048,512]{1,0:T(8,128)(2,1)} %get-tuple-element.7) | data formatting | bytes 4194304
  59.6 0.0 copy-done
  59.7 0.6 copy.24
Async XLA Ops:
  56.6 3.0 %copy-start = (f32[1,512]{1,0:T(1,128)S(1)}, f32[1,512]{1,0:T(1,128)}, u32[]{:S(2)}) copy-start(f32[1,512]{1,0:T(1,128)} %get-tuple-element.8) | copy-start | bytes 6148

commit v2 on v1

v2 whole, which is shorter than its diff:
```python
import functools

import jax
import jax.numpy as jnp
from jax import lax
from jax.experimental import pallas as pl
from jax.experimental.pallas import tpu as pltpu
from jax.sharding import PartitionSpec as P

BF = jnp.bfloat16
F32 = jnp.float32
MESH = pl.DeviceIdType.MESH

GRID_AT, ENC_AT, ES_AT, EF_AT, NF_AT, NS_AT, ROWS = 0, 16, 48, 64, 112, 144, 160
GROUPS = ((0, 64), (64, 112), (112, 160))
PIECES = 31
TILE = 512


def silu(v):
    h = 0.5 * v
    return h + h * jnp.tanh(h)


def dot(a, b):
    return jnp.dot(a, b, preferred_element_type=F32)


def column(row):
    return jnp.broadcast_to(row, (128, 128)).T


def kernel(
    mesh_h, edge_h, gridf_h, snd_h, rcv_h, lists_h, lsrc_h, ltgt_h, area_h,
    gw_h, enc_h, ef_h, es_h, nf_h, ns_h,
    mesh_o, edge_o, mass_o,
    buf, gs, mesh_v, gridf_v, x_v, snd_v, rcv_v, lists_v, lsrc_v, ltgt_v, area_v,
    gt_w, enc_w, r_w, w23, es_w, nf_w, ns_w,
    ol, olt, ort, e1, l0, hs, hr, acol, msrc, asub, fsrc, aface,
    in_sem, w_sem, g_s, g_r, near, far, h_s, h_r, ms_s, ms_r, mf_s, mf_r,
):
    f = lax.axis_index("face")
    s = lax.axis_index("sub")
    c = lax.rem(f, 2)
    y, x = lax.div(s, 4), lax.rem(s, 4)
    b = y + c * (x - y)
    a = x + c * (y - x)
    wa, wb = 1 + 3 * c, 4 - 3 * c
    a_r, a_l, a_2 = lax.rem(a + 1, 4), lax.rem(a + 3, 4), lax.rem(a + 2, 4)
    b_r, b_l, b_2 = lax.rem(b + 1, 4), lax.rem(b + 3, 4), lax.rem(b + 2, 4)
    to_ar, to_al = (f, b * wb + a_r * wa), (f, b * wb + a_l * wa)
    to_br, to_bl = (f, b_r * wb + a * wa), (f, b_l * wb + a * wa)
    sibling = (f + 1 - 2 * c, s)
    other = 1 - c
    z_r, z_l = lax.rem(f + 2, 16), lax.rem(f + 14, 16)
    z_2r, z_2l = lax.rem(f + 4, 16), lax.rem(f + 12, 16)

    loads = []
    for at, rows, ref in (
        (ENC_AT, 32, enc_h), (ES_AT, 16, es_h), (EF_AT, 48, ef_h), (NF_AT, 32, nf_h), (NS_AT, 16, ns_h),
    ):
        n = len(loads)
        loads.append(pltpu.make_async_copy(
            ref.at[pl.ds(c * rows, rows)], buf.at[c, b, a, pl.ds(at, rows)], w_sem.at[n]))
        loads.append(pltpu.make_async_copy(
            ref.at[pl.ds(other * rows, rows)], buf.at[other, a, b, pl.ds(at, rows)], w_sem.at[n + 1]))
    gload = pltpu.make_async_copy(gw_h, gs, w_sem.at[10])
    gload.start()
    for copy in loads:
        copy.start()
    ins = [
        pltpu.make_async_copy(src, dst, in_sem.at[n])
        for n, (src, dst) in enumerate((
            (lsrc_h, lsrc_v), (ltgt_h, ltgt_v), (snd_h, snd_v), (rcv_h, rcv_v), (lists_h, lists_v),
            (area_h, area_v), (gridf_h, gridf_v), (mesh_h, mesh_v), (edge_h, x_v.at[:, pl.ds(0, 512)]),
        ))
    ]
    for copy in ins:
        copy.start()

    barrier = pltpu.get_barrier_semaphore()
    for peer in (
        sibling, to_ar, to_al, to_br, to_bl,
        (z_r, s), (z_l, s), (z_r + 1 - 2 * c, s), (z_l + 1 - 2 * c, s),
    ):
        pl.semaphore_signal(barrier, inc=1, device_id=peer, device_id_type=MESH)

    gload.wait()
    turned = gs[...]
    first, second = turned[0:16], turned[16:32]
    mine = jnp.where(c == 0, first, second)
    theirs = jnp.where(c == 0, second, first)
    pad = jnp.zeros((16, 128), BF)
    buf[c, b, a, 0:16, :] = jnp.concatenate([mine, pad], axis=1)
    buf[other, a, b, 0:16, :] = jnp.concatenate([theirs, pad], axis=1)
    for copy in loads:
        copy.wait()

    pl.semaphore_wait(barrier, 9)

    def remote(src, dst, send, recv, to):
        copy = pltpu.make_async_remote_copy(
            src_ref=src, dst_ref=dst, send_sem=send, recv_sem=recv, device_id=to, device_id_type=MESH)
        return copy

    def same(ref, send, recv, to):
        return remote(ref, ref, send, recv, to)

    class Gather:
        def __init__(self, g):
            self.g, self.used, self.sent = g, 0, []
            rows = pl.ds(GROUPS[g][0], GROUPS[g][1] - GROUPS[g][0])
            col = (a, a_l, a_r, a_2)
            row = (b, b_l, b_r, b_2)

            def piece(i, k, to, half=None):
                ref = buf.at[c, row[i], col[k], rows]
                if half is not None:
                    ref = ref.at[:, pl.ds(256 * half, 256)]
                n = self.used
                self.used += 1
                copy = same(ref, g_s.at[g, n], g_r.at[g, n], to)
                self.sent.append(copy)
                return copy

            self.p1 = [piece(0, 0, to_ar), piece(0, 0, to_al)]
            self.p1f = [piece(0, 1, to_ar, 0), piece(0, 2, to_al, 1)]
            self.p2 = [[piece(0, k, to_br), piece(0, k, to_bl)] for k in range(4)]
            self.p2f = [piece(1, 0, to_br), piece(2, 1, to_bl), piece(2, 2, to_bl), piece(1, 3, to_br)]
            self.dd = {(i, k): piece(i, k, sibling) for i in range(4) for k in range(4) if i or k}

        def send_p1(self):
            start(self.p1)

        def send_p2(self, *ks):
            for k in ks:
                start(self.p2[k])

        def got_p1(self):
            arrived(self.p1)
            start(self.p1f)
            start([self.dd[0, 1], self.dd[0, 2]])

        def got_p1f(self):
            arrived(self.p1f)
            start([self.dd[0, 3]])

        def got_p2(self, *ks):
            for k in ks:
                arrived(self.p2[k])
                start([self.p2f[k], self.dd[1, k], self.dd[2, k]])

        def got_p2f(self, *ks):
            for k in ks:
                arrived([self.p2f[k]])
                start([self.dd[3, k]])

        def done(self):
            arrived(self.dd.values())

    def start(copies):
        for copy in copies:
            copy.start()

    def arrived(copies):
        for copy in copies:
            copy.wait_recv()

    ga, gb, gc = Gather(0), Gather(1), Gather(2)

    ga.send_p1()
    ga.send_p2(0)
    gb.send_p1()
    gc.send_p1()
    for peer in (z_r, z_l):
        pl.semaphore_signal(near, inc=1, device_id=(peer, s), device_id_type=MESH)

    for copy in ins[0:6]:
        copy.wait()
    lanes = lax.broadcasted_iota(jnp.int32, (128, 128), 1).astype(F32)
    node_rows = lax.broadcasted_iota(jnp.int32, (256, 128), 0).astype(F32)

    def hot(col, first):
        return jnp.where(col == lanes + float(first), 1.0, 0.0).astype(BF)

    lsrc = lsrc_v[...].astype(F32)
    ltgt = ltgt_v[...].astype(F32)
    for j in range(4):
        col = column(lsrc[j:j + 1])
        for k in range(2):
            ol[128 * j:128 * (j + 1), 128 * k:128 * (k + 1)] = hot(col, 128 * k)
        col = column(ltgt[j:j + 1])
        for k in range(2):
            ol[128 * j:128 * (j + 1), 256 + 128 * k:256 + 128 * (k + 1)] = hot(col, 128 * k)
        olt[:, 128 * j:128 * (j + 1)] = jnp.where(node_rows == ltgt[j:j + 1], 1.0, 0.0).astype(BF)
    ga.got_p1()
    ga.send_p2(1, 2)
    ga.got_p2(0)
    gb.got_p1()

    snd = snd_v[...].astype(F32)
    rcv = rcv_v[...].astype(F32)

    def edge_hot(js):
        for j in js:
            at = slice(128 * j, 128 * (j + 1))
            col = column(snd[j:j + 1])
            for k in range(2):
                x_v[at, 512 + 128 * k:512 + 128 * (k + 1)] = hot(col, 128 * k)
            x_v[at, 1024:1152] = hot(col, 256)
            col = column(rcv[j:j + 1])
            for k in range(2):
                x_v[at, 768 + 128 * k:768 + 128 * (k + 1)] = hot(col, 128 * k)
            t, o = j // 4, 128 * (j % 4)
            ort[t, :, o:o + 128] = jnp.where(node_rows == rcv[j:j + 1], 1.0, 0.0).astype(BF)

    edge_hot(range(0, 8))
    for j in range(2):
        acol[128 * j:128 * (j + 1), :] = column(area_v[j:j + 1, :])
    ga.got_p1f()
    ga.send_p2(3)
    gb.send_p2(0)
    ga.got_p2(1, 2)
    gb.send_p2(1, 2)
    gc.got_p1()
    edge_hot(range(8, 16))
    ga.got_p2f(0)
    gb.got_p1f()
    ga.got_p2(3)
    gb.send_p2(3)
    gb.got_p2(0)
    gc.send_p2(0)
    pl.semaphore_wait(near, 2)
    for peer in (z_2r, z_2l):
        pl.semaphore_signal(far, inc=1, device_id=(peer, s), device_id_type=MESH)
    ga.got_p2f(1, 2, 3)
    gb.got_p2(1, 2)
    gc.send_p2(1, 2)

    def assemble(at, rows, put):
        for i in range(16):
            put(i * 2 * rows, buf[0, i // 4, i % 4, at:at + rows, :])
            put(i * 2 * rows + rows, buf[1, i % 4, i // 4, at:at + rows, :])

    ga.done()
    for i in range(16):
        gt_w[i * 32:i * 32 + 16, :] = buf[0, i // 4, i % 4, 0:16, 0:384]
        gt_w[i * 32 + 16:i * 32 + 32, :] = buf[1, i % 4, i // 4, 0:16, 0:384]

    def put_enc(at, block):
        enc_w[at:at + block.shape[0], :] = block

    assemble(ENC_AT, 32, put_enc)
    for copy in ins[6:9]:
        copy.wait()

    grid_latent = silu(lax.dot_general(
        gridf_v[...], gt_w[...], (((1,), (1,)), ((), ())), preferred_element_type=F32)).astype(BF)
    from_grid = dot(grid_latent, enc_w[0:512, :]).astype(BF)
    from_mesh = dot(mesh_v[...], enc_w[512:1024, :]).astype(BF)
    messages = silu(dot(ol[...], jnp.concatenate([from_grid, from_mesh], axis=0))).astype(BF)
    l0[...] = (mesh_v[...].astype(F32) + dot(olt[...], messages)).astype(BF)

    slot_rows = lax.broadcasted_iota(jnp.int32, (256, 32), 0)
    for d in range(4):
        pick = jnp.where(slot_rows == lists_v[d:d + 1, :], 1.0, 0.0).astype(BF)
        hs[d] = lax.dot_general(
            pick, l0[...], (((0,), (0,)), ((), ())), preferred_element_type=F32).astype(BF)
    targets = (
        (lax.rem(f + 1, 16), s), (lax.rem(f + 15, 16), s), (f, lax.rem(s + 1, 16)), (f, lax.rem(s + 15, 16)))
    halo = [remote(hs.at[d], hr.at[d], h_s.at[d], h_r.at[d], targets[d]) for d in range(4)]
    start(halo)
    gb.got_p2f(0)
    gc.got_p1f()
    gb.got_p2(3)
    gc.send_p2(3)
    gc.got_p2(0)
    gb.got_p2f(1, 2, 3)
    gb.done()
    gc.got_p2(1, 2)

    def put_ef(at, block):
        done = 0
        while done < block.shape[0]:
            place = at + done
            limit = block.shape[0] - done if place >= 512 else min(block.shape[0] - done, 512 - place)
            if place < 512:
                r_w[place:place + limit, :] = block[done:done + limit]
            else:
                w23[place - 512:place - 512 + limit, :] = block[done:done + limit]
            done += limit

    assemble(EF_AT, 48, put_ef)
    r_w[512:768, :] = dot(l0[...], w23[0:512, :]).astype(BF)
    r_w[768:1024, :] = dot(l0[...], w23[512:1024, :]).astype(BF)
    for t in range(4):
        at = slice(TILE * t, TILE * (t + 1))
        e1[at, :] = dot(x_v[at, 0:1024], r_w[0:1024, :])
        if t == 1:
            gc.got_p2f(0)
            gc.got_p2(3)
    arrived(halo)
    r_w[1024:1152, :] = dot(hr[...].reshape(128, 512), w23[0:512, :]).astype(BF)
    def put_to(ref):
        def put(at, block):
            ref[at:at + block.shape[0], :] = block
        return put

    assemble(ES_AT, 16, put_to(es_w))

    incoming = jnp.zeros((256, 512), F32)
    for t in range(4):
        at = slice(TILE * t, TILE * (t + 1))
        hidden = silu(e1[at, :] + dot(x_v[at, 1024:1152], r_w[1024:1152, :])).astype(BF)
        new = (x_v[at, 0:512].astype(F32) + dot(hidden, es_w[...])).astype(BF)
        edge_o[at, :] = new
        incoming = incoming + dot(ort[t], new)
        if t == 1:
            gc.got_p2f(1, 2)
        if t == 2:
            gc.got_p2f(3)
    gc.done()
    assemble(NF_AT, 32, put_to(nf_w))
    assemble(NS_AT, 16, put_to(ns_w))

    node_hidden = silu(dot(l0[...], nf_w[0:512, :]) + dot(incoming.astype(BF), nf_w[512:1024, :])).astype(BF)
    result = (l0[...].astype(F32) + dot(node_hidden, ns_w[...])).astype(BF)
    mesh_o[...] = result

    wide = result.astype(F32)
    for k in range(4):
        msrc[:, 128 * k:128 * (k + 1)] = jnp.sum(wide[:, 128 * k:128 * (k + 1)] * acol[...], axis=0, keepdims=True)

    def exchange(source, slots, me, peer, sends, recvs):
        slots[me] = source[...]
        copies = [
            remote(source, slots.at[me], sends.at[k - 1], recvs.at[me], peer(lax.rem(me + k, 16)))
            for k in range(1, 16)
        ]
        start(copies)
        for k in range(1, 16):
            j = lax.rem(me + k, 16)
            remote(source, slots.at[j], sends.at[k - 1], recvs.at[j], peer(j)).wait_recv()
        return copies

    pl.semaphore_wait(far, 2)
    by_sub = exchange(msrc, asub, s, lambda j: (f, j), ms_s, ms_r)
    fsrc[...] = jnp.sum(asub[...], axis=0)
    by_face = exchange(fsrc, aface, f, lambda j: (j, s), mf_s, mf_r)
    total = jnp.sum(aface[...], axis=0) / 65536.0
    mass_o[...] = total

    for group in (ga.sent, gb.sent, gc.sent, halo, by_sub, by_face):
        for copy in group:
            copy.wait_send()


def per_device(
    mesh_latent, edge_latent, grid_features, senders, receivers, send_lists, link_sources, link_targets,
    node_area, grid_weight, encode_weight, edge_first, edge_second, node_first, node_second,
):
    dma = pltpu.SemaphoreType.DMA
    vm = pltpu.VMEM
    operands = (
        mesh_latent, edge_latent, grid_features, senders.reshape(16, 128), receivers.reshape(16, 128),
        send_lists[0], link_sources.reshape(4, 128), link_targets.reshape(4, 128), node_area.reshape(2, 128),
        grid_weight.T, encode_weight, edge_first[0], edge_second[0], node_first[0], node_second[0],
    )
    return pl.pallas_call(
        kernel,
        out_shape=(
            pltpu.VMEM((256, 512), BF),
            pltpu.VMEM((2048, 512), BF),
            pltpu.VMEM((1, 512), F32),
        ),
        in_specs=[pl.BlockSpec(memory_space=pltpu.HBM)] * 15,
        out_specs=(
            pl.BlockSpec(memory_space=pltpu.VMEM),
            pl.BlockSpec(memory_space=pltpu.VMEM),
            pl.BlockSpec(memory_space=pltpu.VMEM),
        ),
        scratch_shapes=[
            vm((2, 4, 4, ROWS, 512), BF), vm((32, 384), BF), vm((256, 512), BF), vm((256, 384), BF),
            vm((2048, 1152), BF), vm((16, 128), jnp.int32), vm((16, 128), jnp.int32), vm((4, 32), jnp.int32),
            vm((4, 128), jnp.int32), vm((4, 128), jnp.int32), vm((2, 128), F32),
            vm((512, 384), BF), vm((1024, 512), BF), vm((1152, 512), BF), vm((1024, 512), BF),
            vm((512, 512), BF), vm((1024, 512), BF), vm((512, 512), BF),
            vm((512, 512), BF), vm((256, 512), BF), vm((4, 256, 512), BF), vm((2048, 512), F32),
            vm((256, 512), BF), vm((4, 32, 512), BF), vm((4, 32, 512), BF), vm((256, 128), F32), vm((1, 512), F32), vm((16, 1, 512), F32),
            vm((1, 512), F32), vm((16, 1, 512), F32),
            dma((9,)), dma((11,)), dma((3, PIECES)), dma((3, PIECES)),
            pltpu.SemaphoreType.REGULAR, pltpu.SemaphoreType.REGULAR, dma((4,)), dma((4,)),
            dma((15,)), dma((16,)), dma((15,)), dma((16,)),
        ],
        compiler_params=pltpu.CompilerParams(
            collective_id=0, has_side_effects=True, vmem_limit_bytes=40 * 1024 * 1024),
        cost_estimate=pl.CostEstimate(flops=6_000_000_000, bytes_accessed=6_000_000, transcendentals=1_500_000),
        name="graph_layer",
    )(*(pltpu.with_memory_space_constraint(operand, pltpu.HBM) for operand in operands))


def solution(mesh):
    both = ("face", "sub")
    placed = (
        P(both, None), P(both, None), P(both, None), P(both), P(both), P(both, None, None), P(both), P(both), P(both),
        P(None, "sub"), P("sub", None), P(None, "sub", None), P(None, "sub", None), P(None, "sub", None),
        P(None, "sub", None),
    )
    return jax.shard_map(
        per_device, mesh=mesh, in_specs=placed, out_specs=(P(both, None), P(both, None), P()), check_vma=False)
```

time: 60.5 us -> 52.6 us (0.87)
  local copies, waits for them, and re-layouts: 6.78 us -> 2.6 us
  Pallas kernels: 52.8 us -> 49.2 us
    unnamed x6 -> x3, local copies, waits for them, and re-layouts: 6.78 us -> 2.6 us
    pallas_call x1, Pallas kernels: 52.8 us -> 49.2 us  [per_device(): pl.pallas_call(kernel, out_shape=(pltpu.VMEM((256, 512), BF), pltpu.VMEM(...]
where the time goes in v2:
time: 52.6 us; the launch traced here: 52.4 us
  Pallas kernels  49.2 us (94%)
  local copies, waits for them, and re-layouts  2.6 us (5%)
  between operations  0.65 us (1%)
    pallas_call x1, Pallas kernels, per_device(): pl.pallas_call(kernel, out_shape=(pltpu.VMEM((256, 512), BF), pltpu.VMEM(...  49.2 us
    unnamed x3, local copies, waits for them, and re-layouts  2.6 us

profile of v2, /device:TPU:1, one launch (start us, length us, event | category | flops | bytes accessed | tf_op | source)
XLA Modules:
  0.0 52.4 jit_solution(10294387531417303529)
XLA Ops:
  0.6 49.2 %graph_layer.1 = (bf16[256,512]{1,0:T(8,128)(2,1)S(1)}, bf16[2048,512]{1,0:T(8,128)(2,1)S(1)}, f32[1,512]{1,0:T(1,128)S(1)}) custom-call(bf16[256,512]{1,0:T(8,128)(2,1)} %mesh_h.1, bf16[2048,512]{1,0:T(8,128)(2,1)} %edge_h.1, bf16[256,384]{1,0:T(8,128)(2,1)} %gridf_h.1, s32[16,128]{1,0:T(8,128)} %bitcast.16, s32[16,128]{1,0:T(8,128)} %bitcast.17, ...), custom_call_target="tpu_custom_call" | custom-call | flops 6000000000 | bytes 6000000 | tf_op jit(solution)/shard_map/graph_layer/pallas_call | solution.py:369
  49.8 0.7 %copy.21 = bf16[256,512]{1,0:T(8,128)(2,1)} copy(bf16[256,512]{1,0:T(8,128)(2,1)S(1)} %get-tuple-element.3) | data formatting | bytes 524288
  50.5 0.6 %copy.23 = f32[1,512]{1,0:T(1,128)} copy(f32[1,512]{1,0:T(1,128)S(1)} %get-tuple-element.5) | data formatting | bytes 4096
  51.1 1.3 %copy.22 = bf16[2048,512]{1,0:T(8,128)(2,1)} copy(bf16[2048,512]{1,0:T(8,128)(2,1)S(1)} %get-tuple-element.4) | data formatting | bytes 4194304
